TPU v7x, 32 devices: a whole 2x2x4 slice. The times are simulated.
32 devices in a mesh: parts: 2 (over y), rng: 8 (over z, x), chan: 2 (over core).
Axes of the slice: x: 2, y: 2, z: 4, core: 2. Of those that a mesh axis runs over, the one named last changes fastest.
Arguments:
- snapshots: bfloat16 [8, 2, 16384, 192], P('parts', None, 'rng', 'chan'), parts along dimension 0, may hold values from -24 to 24
- train_gates: int32 [8, 128], P('parts', 'rng'), parts along dimension 0, may hold values from 0 to 2047
- guard_keep: int32 [8, 128], P('parts', 'rng'), parts along dimension 0, may hold values 0 or 1
- beam_cells: int32 [8, 16], P('parts'), parts along dimension 0, may hold values from 0 to 767
Outputs:
- beam_out: bfloat16 [8, 2, 16, 16384], P('parts', None, None, ('rng', 'chan')), parts along dimension 0
- weights: float32 [8, 16, 384], P('parts'), parts along dimension 0
There are 2 independent parts, one for each index of `parts`. A program takes and returns all parts, laid end to end along the dimension named above; each array names one. Nothing has to cross between parts.
Inputs may be any that keep to these rules, and one draw needn't show every extreme that they name: `train_gates`: an offset into the 2048 gates of the range group that holds the entry. `beam_cells`: angle cell times 12 plus Doppler cell.
All inputs are finite; a program needn't handle non-finite values. No bound on the sum of `guard_keep` on one device may be relied on, other than what follows from the above.
Results may differ from a plain program's by a relative error of at most 0.01225.
Values may be sent and summed in bfloat16 or wider, within the bound.
A program may use at most 64 MiB of HBM per device.

v0:
```python
import math
import jax
import jax.numpy as jnp
from jax import lax
from jax.sharding import PartitionSpec as P

ELEM = 16
PULSE = 12
CH = 192
ANGLES = 64
LOADING = 0.05


def steering(cells):
    angle_cell = (cells // PULSE).astype(jnp.float32)
    doppler_cell = (cells % PULSE).astype(jnp.float32)
    sine_angle = -1.0 + (2.0 * angle_cell + 1.0) / ANGLES
    doppler_freq = (doppler_cell + 0.5) / PULSE - 0.5
    channel = jnp.arange(CH, dtype=jnp.int32)
    element = (channel % ELEM).astype(jnp.float32)
    pulse_index = (channel // ELEM).astype(jnp.float32)
    phases = (
        math.pi * element[None, :] * sine_angle[:, None]
        + 2.0 * math.pi * pulse_index[None, :] * doppler_freq[:, None]
    )
    norm_scale = 1.0 / math.sqrt(CH)
    return jnp.concatenate([jnp.cos(phases), jnp.sin(phases)], axis=1) * norm_scale


def gram_product(left, right):
    return lax.dot_general(
        left, right, (((0,), (0,)), ((), ())), preferred_element_type=jnp.float32
    )


def apply_taps(beam_taps, samples):
    return lax.dot_general(
        beam_taps, samples, (((0,), (1,)), ((), ())), preferred_element_type=jnp.float32
    )


def solve_weights(covariance, steer_vec):
    matrix_order = covariance.shape[0]
    loading = LOADING * jnp.trace(covariance) / matrix_order + 1e-06
    loaded = covariance + loading * jnp.eye(matrix_order, dtype=jnp.float32)
    factor = jnp.linalg.cholesky(loaded)
    forward = lax.linalg.triangular_solve(factor, steer_vec.T, left_side=True, lower=True)
    solved = lax.linalg.triangular_solve(
        factor, forward, left_side=True, lower=True, transpose_a=True
    )
    unit_gain = jnp.sum(steer_vec.T * solved, axis=0)
    return (solved / unit_gain[None, :]).T


def make_taps(weight_rows):
    weights = weight_rows.T
    half_order = weights.shape[0] // 2
    rotated = jnp.concatenate([-weights[half_order:], weights[:half_order]], axis=0)
    return jnp.concatenate([weights, rotated], axis=1).astype(jnp.bfloat16)


def per_device(snapshots, train_gates, guard_keep, beam_cells):
    groups = snapshots.shape[0]
    shard_width = snapshots.shape[3]
    chan_count = lax.axis_size("chan")
    chan_place = lax.axis_index("chan")
    full_width = shard_width * chan_count
    beam_count = beam_cells.shape[1]
    picked = jax.vmap(lambda cube, chosen: jnp.take(cube, chosen, axis=1))(snapshots, train_gates)
    picked = picked * guard_keep[:, None, :, None].astype(jnp.bfloat16)
    training = lax.all_gather(picked, "chan", axis=3, tiled=True)
    training = lax.all_gather(training, "rng", axis=2, tiled=True)
    cov_list = []
    for bin_group in range(groups):
        chosen = training[bin_group]
        direct = jnp.concatenate([chosen[0], chosen[1]], axis=1)
        turned = jnp.concatenate([-chosen[1], chosen[0]], axis=1)
        covariance = gram_product(direct, direct) + gram_product(turned, turned)
        cov_list.append(covariance)
    cov_stack = jnp.stack(cov_list)
    steer_stack = jax.vmap(steering)(beam_cells)
    rng_place = lax.axis_index("rng")
    group_pick = rng_place % groups
    own_cov = lax.dynamic_index_in_dim(cov_stack, group_pick, 0, keepdims=False)
    own_steer = lax.dynamic_index_in_dim(steer_stack, group_pick, 0, keepdims=False)
    own_weights = solve_weights(own_cov, own_steer)
    group_ids = jnp.arange(groups, dtype=jnp.int32)
    owner = jnp.where((group_ids == group_pick) & (rng_place < groups), 1.0, 0.0).astype(
        jnp.float32
    )
    weight_stack = lax.psum(owner[:, None, None] * own_weights[None], "rng")
    taps_stack = jax.vmap(make_taps)(weight_stack)
    beam_list = []
    for bin_group in range(groups):
        beam_taps = taps_stack[bin_group]
        real_taps = lax.dynamic_slice_in_dim(beam_taps, chan_place * shard_width, shard_width, 0)
        imag_taps = lax.dynamic_slice_in_dim(
            beam_taps, full_width + chan_place * shard_width, shard_width, 0
        )
        partial_out = apply_taps(real_taps, snapshots[bin_group, 0]) + apply_taps(
            imag_taps, snapshots[bin_group, 1]
        )
        outputs = lax.psum_scatter(partial_out, "chan", scatter_dimension=1, tiled=True)
        beam_list.append(outputs.reshape(2, beam_count, outputs.shape[1]).astype(jnp.bfloat16))
    return (jnp.stack(beam_list), weight_stack)


def solution(mesh):
    placed = (
        P("parts", None, "rng", "chan"),
        P("parts", "rng"),
        P("parts", "rng"),
        P("parts", None),
    )
    return jax.shard_map(
        per_device,
        mesh=mesh,
        in_specs=placed,
        out_specs=(P("parts", None, None, ("rng", "chan")), P("parts", None, None)),
        check_vma=False,
    )
```

profile of v0, /device:TPU:0, one launch (start us, length us, event | category | flops | bytes accessed | tf_op | source)
XLA Modules:
  0.0 298.7 jit_solution(11843807177407830651)
XLA Ops:
  7.2 0.7 bitcast_or_fusion
  7.9 0.7 compare_and_fusion
  8.6 11.0 %copy.52 = bf16[4,2,2048,96]{3,1,2,0:T(2,128)(2,1)} copy(bf16[4,2,2048,96]{2,3,1,0:T(8,128)(2,1)} %param.4) | data formatting | bytes 6291456 | tf_op args[0]
  19.7 2.9 gather_fusion
  22.9 2.2 all_gather.6
  25.4 33.1 %all_gather.7 = bf16[4,2,128,192]{3,0,1,2:T(4,128)(2,1)S(1)} all-gather(bf16[4,2,16,192]{3,0,1,2:T(4,128)(2,1)S(1)} %copy.55), channel_id=1, replica_groups=mesh['parts'=2,'rng'=8,'chan'=2] {'rng'}, dimensions={2}, use_global_device_ids=true | all-gather | bytes 442368 | tf_op jit(solution)/shard_map/all_gather | solution.py:72
  58.5 0.8 fusion.132
  63.0 0.7 fusion.8
  64.7 11.7 %cholesky.76 = f32[128,128]{1,0:T(8,128)S(1)} custom-call(f32[128,128]{1,0:T(8,128)S(1)} %cholesky.189), custom_call_target="Cholesky" | custom-call | tf_op jit(solution)/shard_map/jit(cholesky)/cholesky | solution.py:46
  76.5 9.8 %custom-call.24 = f32[1,128,128]{1,2,0:T(8,128)S(1)} custom-call(f32[1,128,128]{2,1,0:T(8,128)S(1)} %get-tuple-element.51), custom_call_target="InvertDiagBlocksLowerTriangular" | custom-call | tf_op jit(solution)/shard_map/jit(cholesky)/cholesky | solution.py:46
  86.9 11.9 %cholesky.160 = f32[128,128]{1,0:T(8,128)S(1)} custom-call(f32[128,128]{1,0:T(8,128)S(1)} %cholesky.193), custom_call_target="Cholesky" | custom-call | tf_op jit(solution)/shard_map/jit(cholesky)/cholesky | solution.py:46
  99.1 9.8 %custom-call.25 = f32[1,128,128]{1,2,0:T(8,128)S(1)} custom-call(f32[1,128,128]{2,1,0:T(8,128)S(1)} %get-tuple-element.49), custom_call_target="InvertDiagBlocksLowerTriangular" | custom-call | tf_op jit(solution)/shard_map/jit(cholesky)/cholesky | solution.py:46
  109.3 0.8 copy-done.1
  110.1 1.4 convolution_subtract_fusion.1
  111.5 11.7 %cholesky.179 = f32[128,128]{1,0:T(8,128)S(1)} custom-call(f32[128,128]{1,0:T(8,128)S(1)} %convolution_subtract_fusion.1), custom_call_target="Cholesky" | custom-call | tf_op jit(solution)/shard_map/jit(cholesky)/cholesky | solution.py:46
  123.4 0.6 compare_reduce_fusion
  124.0 0.6 constant_dynamic-update-slice_fusion.1
  124.6 0.7 compare_reduce_fusion.1
  127.2 1.9 select_select_fusion
  129.1 9.3 %while.1 = (s32[]{:T(128)}, f32[384,384]{0,1:T(8,128)}, s32[3,2]{0,1:T(2,128)S(1)}, f32[3,128,128]{2,1,0:T(8,128)S(1)}, s32[]{:T(128)}) while((s32[]{:T(128)}, f32[384,384]{0,1:T(8,128)}, s32[3,2]{0,1:T(2,128)S(1)}, f32[3,128,128]{2,1,0:T(8,128)S(1)}, s32[]{:T(128)}) %tuple.43), condition=%wide.while_cond, body=%wide.while_body.sunk | while | flops 2 | bytes 393321 | solution.py:48
  129.8 2.3 dynamic-slice.15
  132.3 0.6 fusion.143
  132.9 2.3 dynamic-slice.15
  135.5 0.6 fusion.143
  136.1 2.3 dynamic-slice.15
  138.5 29.5 %custom-call.26 = f32[3,128,128]{1,2,0:T(8,128)S(1)} custom-call(f32[3,128,128]{2,1,0:T(8,128)S(1)} %get-tuple-element.9), custom_call_target="InvertDiagBlocksLowerTriangular" | custom-call | tf_op jit(solution)/shard_map/triangular_solve | solution.py:48
  168.6 1.0 convolution_subtract_fusion.5
  169.8 1.1 convolution_subtract_fusion.4
  171.3 1.0 convolution_subtract_fusion.3
  172.5 1.1 convolution_subtract_fusion.2
  174.1 0.7 broadcast_multiply_fusion
  174.9 71.2 %all-reduce.3.cloned.1.call-done = f32[4,16,384]{2,1,0:T(8,128)} async-done(((f32[4,16,384]{2,1,0:T(8,128)}), f32[4,16,384]{2,1,0:T(8,128)}) %all-reduce.3.cloned.1.call-update) | async-done | bytes 98320 | tf_op jit(solution)/shard_map/psum | solution.py:91
  246.1 0.9 bitcast_convert_fusion
  247.1 0.9 fusion.62
  248.3 1.0 convolution_add_fusion.3
  249.7 1.0 convolution_add_fusion.2
  250.9 1.0 convolution_add_fusion.1
  252.2 1.0 convolution_add_fusion
  253.2 3.1 %reduce-scatter.5.cloned.1.call-done = f32[32,1024]{1,0:T(8,128)} async-done(((f32[32,2048]{1,0:T(8,128)}), f32[32,1024]{1,0:T(8,128)}) %reduce-scatter.5.cloned.1.call-update) | async-done | bytes 131088 | tf_op jit(solution)/shard_map/reduce_scatter | solution.py:103
  256.3 0.9 convert_element_type.85
  257.2 10.2 %reduce-scatter.7.cloned.1.call-done = f32[32,1024]{1,0:T(8,128)} async-done(((f32[32,2048]{1,0:T(8,128)}), f32[32,1024]{1,0:T(8,128)}) %reduce-scatter.7.cloned.1.call-update) | async-done | bytes 131088 | tf_op jit(solution)/shard_map/reduce_scatter | solution.py:103
  267.4 0.9 convert_element_type.87
  268.3 10.1 %reduce-scatter.9.cloned.1.call-done = f32[32,1024]{1,0:T(8,128)} async-done(((f32[32,2048]{1,0:T(8,128)}), f32[32,1024]{1,0:T(8,128)}) %reduce-scatter.9.cloned.1.call-update) | async-done | bytes 131088 | tf_op jit(solution)/shard_map/reduce_scatter | solution.py:103
  278.4 0.9 convert_element_type.89
  279.3 10.6 %reduce-scatter.11.cloned.1.call-done = f32[32,1024]{1,0:T(8,128)} async-done(((f32[32,2048]{1,0:T(8,128)}), f32[32,1024]{1,0:T(8,128)}) %reduce-scatter.11.cloned.1.call-update) | async-done | bytes 131088 | tf_op jit(solution)/shard_map/reduce_scatter | solution.py:103
  289.9 0.9 convert_element_type.91
  290.8 0.7 pad_maximum_fusion
  291.6 0.6 copy.96
  (100 shorter events, 10.4 us)
Async XLA Ops:
  7.2 239.0 %all-reduce.3.cloned.1.call-start = ((), (), s32[]{:S(2)}) async-start(), calls=%async_computation.4 | async-start | bytes 196608 | tf_op jit(solution)/shard_map/psum | solution.py:91
  8.6 14.0 %copy-start.5 = (s32[4,16]{1,0:T(4,128)S(1)}, s32[4,16]{1,0:T(4,128)}, u32[]{:S(2)}) copy-start(s32[4,16]{1,0:T(4,128)} %param.6) | copy-start | bytes 772
  64.7 44.3 %copy-start.2 = (f32[384,384]{1,0:T(8,128)}, f32[384,384]{1,0:T(8,128)S(1)}, u32[]{:S(2)}) copy-start(f32[384,384]{1,0:T(8,128)S(1)} %fusion.7) | copy-start | bytes 1769476
  86.6 81.4 %copy-start.4 = (s32[4,16]{1,0:T(4,128)S(1)}, s32[4,16]{1,0:T(4,128)}, u32[]{:S(2)}) copy-start(s32[4,16]{1,0:T(4,128)} %param.7) | copy-start | bytes 772
  109.3 0.8 copy-start.1
  110.1 138.0 %copy-start = (bf16[4,2,2048,96]{2,3,1,0:T(8,128)(2,1)S(1)}, bf16[4,2,2048,96]{2,3,1,0:T(8,128)(2,1)}, u32[]{:S(2)}) copy-start(bf16[4,2,2048,96]{2,3,1,0:T(8,128)(2,1)} %param.4) | copy-start | bytes 9437188
  174.9 81.4 %reduce-scatter.5.cloned.1.call-start = ((), (), s32[]{:S(2)}) async-start(), calls=%async_computation.5 | async-start | bytes 393216 | tf_op jit(solution)/shard_map/reduce_scatter | solution.py:103
  249.3 18.1 %reduce-scatter.7.cloned.1.call-start = ((), (), s32[]{:S(2)}) async-start(), calls=%async_computation.6 | async-start | bytes 393216 | tf_op jit(solution)/shard_map/reduce_scatter | solution.py:103
  249.6 41.9 %copy-start.3 = (f32[4,16,384]{2,1,0:T(8,128)S(1)}, f32[4,16,384]{2,1,0:T(8,128)}, u32[]{:S(2)}) copy-start(f32[4,16,384]{2,1,0:T(8,128)} %all-reduce.3.cloned.1.call-done) | copy-start | bytes 294916
  250.6 27.7 %reduce-scatter.9.cloned.1.call-start = ((), (), s32[]{:S(2)}) async-start(), calls=%async_computation.7 | async-start | bytes 393216 | tf_op jit(solution)/shard_map/reduce_scatter | solution.py:103
  251.9 38.0 %reduce-scatter.11.cloned.1.call-start = ((), (), s32[]{:S(2)}) async-start(), calls=%async_computation.8 | async-start | bytes 393216 | tf_op jit(solution)/shard_map/reduce_scatter | solution.py:103
Sparse Core Ops, SparseCore 0:
  175.0 71.1 all-reduce.2
  249.5 6.7 reduce-scatter.4
  258.5 8.8 reduce-scatter.6
  269.5 8.8 reduce-scatter.8
  281.0 8.8 reduce-scatter.10
where the time goes:
time: 300 us; the launch traced here: 299 us
  waiting for transfers between devices  105 us (35%)
  other arithmetic  97.9 us (33%)
  blocking collectives  35.3 us (12%)
  local copies, waits for them, and re-layouts  28.6 us (10%)
  between operations  16.8 us (6%)
  matrix products  14.6 us (5%)
    psum x1, waiting for transfers between devices, per_device(): weight_stack = lax.psum(owner[:, None, None] * own_weights[None], 'rng')  71.2 us
    another operation x10, other arithmetic, solve_weights(): factor = jnp.linalg.cholesky(loaded)  56.3 us
    reduce_scatter x4, waiting for transfers between devices, per_device(): lax.psum_scatter(partial_out, 'chan', scatter_dimension=1, tiled=True)  33.9 us
    all_gather x1, blocking collectives, per_device(): training = lax.all_gather(training, 'rng', axis=2, tiled=True)  33.1 us
    another operation x3, other arithmetic, solve_weights(): lax.linalg.triangular_solve(factor, forward, left_side=True, lower=True,...  31.4 us
    unnamed x22, local copies, waits for them, and re-layouts  13.5 us
    another operation x15, local copies, waits for them, and re-layouts  9.25 us
  transfers between devices with their start and end apart: 5, of which 5 were waited for; matrix products, arithmetic and copies ran while one was open for 2% of the time, Pallas kernels for 0%

commit v1 on v0

--- a/solution.py
+++ b/solution.py
@@ -88,7 +88,7 @@
     owner = jnp.where((group_ids == group_pick) & (rng_place < groups), 1.0, 0.0).astype(
         jnp.float32
     )
-    weight_stack = lax.psum(owner[:, None, None] * own_weights[None], "rng")
+    weight_stack = jnp.sum(lax.all_gather(owner[:, None, None] * own_weights[None], "rng"), axis=0)
     taps_stack = jax.vmap(make_taps)(weight_stack)
     beam_list = []
     for bin_group in range(groups):

time: 300 us -> 261 us (0.87)
  waiting for transfers between devices: 105 us -> 34.6 us
  blocking collectives: 35.3 us -> 69.5 us
    psum x1 -> x0, waiting for transfers between devices: 71.2 us -> none  [per_device(): weight_stack = lax.psum(owner[:, None, None] * own_weights[None], 'rng')]
    all_gather x0 -> x1, blocking collectives: none -> 34.2 us  [per_device(): lax.all_gather(owner[:, None, None] * own_weights[None], 'rng')]
    unnamed x22 -> x17, local copies, waits for them, and re-layouts: 13.5 us -> 12.1 us
  transfers between devices with their start and end apart: 5 -> 4, of which waited for: 5 -> 4; matrix products, arithmetic and copies ran while one was open for 2% -> 3% of each run, Pallas kernels for 0% -> 0%
where the time goes in v1:
time: 261 us; the launch traced here: 260 us
  other arithmetic  95.7 us (37%)
  blocking collectives  69.5 us (27%)
  waiting for transfers between devices  34.6 us (13%)
  local copies, waits for them, and re-layouts  26.8 us (10%)
  between operations  16.8 us (6%)
  matrix products  16.4 us (6%)
    another operation x10, other arithmetic, solve_weights(): factor = jnp.linalg.cholesky(loaded)  56.4 us
    reduce_scatter x4, waiting for transfers between devices, per_device(): lax.psum_scatter(partial_out, 'chan', scatter_dimension=1, tiled=True)  34.5 us
    all_gather x1, blocking collectives, per_device(): lax.all_gather(owner[:, None, None] * own_weights[None], 'rng')  34.2 us
    all_gather x1, blocking collectives, per_device(): training = lax.all_gather(training, 'rng', axis=2, tiled=True)  33.1 us
    another operation x3, other arithmetic, solve_weights(): lax.linalg.triangular_solve(factor, forward, left_side=True, lower=True,...  30.4 us
    unnamed x17, local copies, waits for them, and re-layouts  12.1 us
    another operation x15, local copies, waits for them, and re-layouts  8.93 us
    dot_general x8, matrix products, apply_taps(): lax.dot_general(beam_taps, samples, (((0,), (1,)), ((), ())), preferred_e...  7.72 us
  transfers between devices with their start and end apart: 4, of which 4 were waited for; matrix products, arithmetic and copies ran while one was open for 3% of the time, Pallas kernels for 0%

profile of v1, /device:TPU:0, one launch (start us, length us, event | category | flops | bytes accessed | tf_op | source)
XLA Modules:
  0.0 260.1 jit_solution(4678703121463867750)
XLA Ops:
  7.2 0.7 bitcast_or_fusion
  7.9 0.7 compare_and_fusion
  8.6 11.0 %copy.52 = bf16[4,2,2048,96]{3,1,2,0:T(2,128)(2,1)} copy(bf16[4,2,2048,96]{2,3,1,0:T(8,128)(2,1)} %param.4) | data formatting | bytes 6291456 | tf_op args[0]
  19.7 2.9 %gather_fusion = bf16[64,2,96]{2,1,0:T(2,128)(2,1)S(1)} fusion(bf16[4,2,2048,96]{3,1,2,0:T(2,128)(2,1)} %copy.52, s32[64]{0:T(128)S(1)} %reshape.177), kind=kCustom, calls=%fused_computation | custom fusion | bytes 49664 | tf_op jit(solution)/shard_map/vmap(jit(_take))/gather | solution.py:69
  22.9 2.2 all_gather.10
  25.4 33.1 %all_gather.11 = bf16[4,2,128,192]{3,0,1,2:T(4,128)(2,1)S(1)} all-gather(bf16[4,2,16,192]{3,0,1,2:T(4,128)(2,1)S(1)} %copy.55), channel_id=1, replica_groups=mesh['parts'=2,'rng'=8,'chan'=2] {'rng'}, dimensions={2}, use_global_device_ids=true | all-gather | bytes 442368 | tf_op jit(solution)/shard_map/all_gather | solution.py:72
  58.5 0.8 fusion.132
  63.0 0.7 fusion.8
  64.7 11.7 %cholesky.76 = f32[128,128]{1,0:T(8,128)S(1)} custom-call(f32[128,128]{1,0:T(8,128)S(1)} %cholesky.189), custom_call_target="Cholesky" | custom-call | tf_op jit(solution)/shard_map/jit(cholesky)/cholesky | solution.py:46
  76.5 9.8 %custom-call.24 = f32[1,128,128]{1,2,0:T(8,128)S(1)} custom-call(f32[1,128,128]{2,1,0:T(8,128)S(1)} %get-tuple-element.51), custom_call_target="InvertDiagBlocksLowerTriangular" | custom-call | tf_op jit(solution)/shard_map/jit(cholesky)/cholesky | solution.py:46
  86.9 11.9 %cholesky.160 = f32[128,128]{1,0:T(8,128)S(1)} custom-call(f32[128,128]{1,0:T(8,128)S(1)} %cholesky.193), custom_call_target="Cholesky" | custom-call | tf_op jit(solution)/shard_map/jit(cholesky)/cholesky | solution.py:46
  99.1 9.8 %custom-call.25 = f32[1,128,128]{1,2,0:T(8,128)S(1)} custom-call(f32[1,128,128]{2,1,0:T(8,128)S(1)} %get-tuple-element.49), custom_call_target="InvertDiagBlocksLowerTriangular" | custom-call | tf_op jit(solution)/shard_map/jit(cholesky)/cholesky | solution.py:46
  109.3 0.4 convolution_subtract_fusion.1
  109.7 11.7 %cholesky.179 = f32[128,128]{1,0:T(8,128)S(1)} custom-call(f32[128,128]{1,0:T(8,128)S(1)} %convolution_subtract_fusion.1), custom_call_target="Cholesky" | custom-call | tf_op jit(solution)/shard_map/jit(cholesky)/cholesky | solution.py:46
  121.5 0.7 compare_reduce_fusion
  122.3 0.6 compare_reduce_fusion.1
  124.8 0.9 select_select_fusion
  125.7 9.0 %while.1 = (s32[]{:T(128)}, f32[384,384]{0,1:T(8,128)}, s32[3,2]{0,1:T(2,128)S(1)}, f32[3,128,128]{2,1,0:T(8,128)S(1)}, s32[]{:T(128)}) while((s32[]{:T(128)}, f32[384,384]{0,1:T(8,128)}, s32[3,2]{0,1:T(2,128)S(1)}, f32[3,128,128]{2,1,0:T(8,128)S(1)}, s32[]{:T(128)}) %tuple.43), condition=%wide.while_cond, body=%wide.while_body.sunk | while | flops 2 | bytes 393321 | solution.py:48
  125.7 0.5 fusion.143
  126.3 2.5 dynamic-slice.15
  129.0 0.5 fusion.143
  129.5 2.2 dynamic-slice.15
  131.9 0.5 fusion.143
  132.4 2.1 dynamic-slice.15
  134.7 29.5 %custom-call.26 = f32[3,128,128]{1,2,0:T(8,128)S(1)} custom-call(f32[3,128,128]{2,1,0:T(8,128)S(1)} %get-tuple-element.9), custom_call_target="InvertDiagBlocksLowerTriangular" | custom-call | tf_op jit(solution)/shard_map/triangular_solve | solution.py:48
  164.2 0.3 fusion.69
  164.8 1.0 convolution_subtract_fusion.5
  166.0 1.1 convolution_subtract_fusion.4
  167.4 1.1 convolution_subtract_fusion.3
  168.7 1.1 convolution_subtract_fusion.2
  170.4 34.2 %all_gather.12 = f32[8,4,16,384]{3,2,1,0:T(8,128)} all-gather(f32[1,4,16,384]{3,2,1,0:T(8,128)S(1)} %broadcast_multiply_fusion), channel_id=1, replica_groups=mesh['parts'=2,'rng'=8,'chan'=2] {'rng'}, dimensions={0}, use_global_device_ids=true | all-gather | bytes 884736 | tf_op jit(solution)/shard_map/all_gather | solution.py:91
  204.6 1.2 reduce_sum.30
  206.0 0.6 fusion.133
  206.7 1.0 fusion.19
  207.6 1.7 convolution_add_fusion.3
  209.4 1.0 fusion.16
  210.3 1.7 convolution_add_fusion.2
  212.3 1.0 convolution_add_fusion.1
  213.6 1.0 convolution_add_fusion
  214.6 3.5 %reduce-scatter.5.cloned.1.call-done = f32[32,1024]{1,0:T(8,128)} async-done(((f32[32,2048]{1,0:T(8,128)}), f32[32,1024]{1,0:T(8,128)}) %reduce-scatter.5.cloned.1.call-update) | async-done | bytes 131088 | tf_op jit(solution)/shard_map/reduce_scatter | solution.py:103
  218.1 0.9 convert_element_type.85
  219.0 10.2 %reduce-scatter.7.cloned.1.call-done = f32[32,1024]{1,0:T(8,128)} async-done(((f32[32,2048]{1,0:T(8,128)}), f32[32,1024]{1,0:T(8,128)}) %reduce-scatter.7.cloned.1.call-update) | async-done | bytes 131088 | tf_op jit(solution)/shard_map/reduce_scatter | solution.py:103
  229.2 0.9 convert_element_type.87
  230.1 10.2 %reduce-scatter.9.cloned.1.call-done = f32[32,1024]{1,0:T(8,128)} async-done(((f32[32,2048]{1,0:T(8,128)}), f32[32,1024]{1,0:T(8,128)}) %reduce-scatter.9.cloned.1.call-update) | async-done | bytes 131088 | tf_op jit(solution)/shard_map/reduce_scatter | solution.py:103
  240.4 0.9 convert_element_type.89
  241.3 10.6 %reduce-scatter.11.cloned.1.call-done = f32[32,1024]{1,0:T(8,128)} async-done(((f32[32,2048]{1,0:T(8,128)}), f32[32,1024]{1,0:T(8,128)}) %reduce-scatter.11.cloned.1.call-update) | async-done | bytes 131088 | tf_op jit(solution)/shard_map/reduce_scatter | solution.py:103
  251.9 0.9 convert_element_type.91
  252.8 0.7 pad_maximum_fusion
  (94 shorter events, 9.0 us)
Async XLA Ops:
  7.2 211.0 %reduce-scatter.5.cloned.1.call-start = ((), (), s32[]{:S(2)}) async-start(), calls=%async_computation.4 | async-start | bytes 393216 | tf_op jit(solution)/shard_map/reduce_scatter | solution.py:103
  8.6 14.0 %copy-start.3 = (s32[4,16]{1,0:T(4,128)S(1)}, s32[4,16]{1,0:T(4,128)}, u32[]{:S(2)}) copy-start(s32[4,16]{1,0:T(4,128)} %param.6) | copy-start | bytes 772
  86.6 77.6 %copy-start.2 = (s32[4,16]{1,0:T(4,128)S(1)}, s32[4,16]{1,0:T(4,128)}, u32[]{:S(2)}) copy-start(s32[4,16]{1,0:T(4,128)} %param.7) | copy-start | bytes 772
  125.7 81.0 %copy-start = (bf16[4,2,2048,96]{2,3,1,0:T(8,128)(2,1)S(1)}, bf16[4,2,2048,96]{2,3,1,0:T(8,128)(2,1)}, u32[]{:S(2)}) copy-start(bf16[4,2,2048,96]{2,3,1,0:T(8,128)(2,1)} %param.4) | copy-start | bytes 9437188
  205.8 7.5 %copy-start.1 = (f32[4,16,384]{2,1,0:T(8,128)}, f32[4,16,384]{2,1,0:T(8,128)S(1)}, u32[]{:S(2)}) copy-start(f32[4,16,384]{2,1,0:T(8,128)S(1)} %reduce_sum.30) | copy-start | bytes 294916
  209.3 19.9 %reduce-scatter.7.cloned.1.call-start = ((), (), s32[]{:S(2)}) async-start(), calls=%async_computation.5 | async-start | bytes 393216 | tf_op jit(solution)/shard_map/reduce_scatter | solution.py:103
  212.0 28.3 %reduce-scatter.9.cloned.1.call-start = ((), (), s32[]{:S(2)}) async-start(), calls=%async_computation.6 | async-start | bytes 393216 | tf_op jit(solution)/shard_map/reduce_scatter | solution.py:103
  213.3 38.6 %reduce-scatter.11.cloned.1.call-start = ((), (), s32[]{:S(2)}) async-start(), calls=%async_computation.7 | async-start | bytes 393216 | tf_op jit(solution)/shard_map/reduce_scatter | solution.py:103
Sparse Core Ops, SparseCore 0:
  209.4 8.6 reduce-scatter.4
  220.3 8.8 reduce-scatter.6
  231.5 8.8 reduce-scatter.8
  243.0 8.8 reduce-scatter.10
